TPU v7x, 32 devices: a whole 2x2x4 slice. The times are simulated.
32 devices in a mesh: seq: 8 (over z, x), mp: 4 (over y, core).
Axes of the slice: x: 2, y: 2, z: 4, core: 2. Of those that a mesh axis runs over, the one named last changes fastest.
Arguments:
- grad_rows: bfloat16 [4096, 8192], P('seq', 'mp'), may hold values from -6 to 6
- img_start: int32 [64], replicated, may hold values from 0 to 4092, as said below
- img_len: int32 [64], replicated, may hold values from 4 to 64, as said below
- img_owner: int32 [64], replicated, may hold values from 0 to 7, as said below
- pre_act: bfloat16 [4096, 5120], P('seq', 'mp'), may hold values from -6 to 6
- w_out: bfloat16 [5120, 8192], P(None, 'mp'), may hold values from -0.0625 to 0.0625
Outputs:
- pre_grad: bfloat16 [4096, 5120], P('seq', 'mp')
- weight_grad: bfloat16 [5120, 8192], P('seq', 'mp')
Inputs may be any that keep to these rules, and one draw needn't show every extreme that they name: Image i lies inside positions i * 64 to (i + 1) * 64 - 1: img_start[i] - i * 64 + img_len[i] <= 64. `img_len`: A multiple of 4. In every draw some owner has all its images of exactly 64 merged tokens. `img_owner`: the images i with one value of i % 8 all have different owners, and so do the 8 images of one stripe (images i with one value of i // 8).
All inputs are finite; a program needn't handle non-finite values.
Results may differ from a plain program's by a relative error of at most 0.02.
Values may be sent and summed in bfloat16 or wider, within the bound.
A program may use at most 192 MiB of HBM per device.

v0:
```python
import functools
import math

import jax
import jax.numpy as jnp
from jax import lax
from jax.experimental import pallas as pl
from jax.experimental.pallas import tpu as pltpu
from jax.sharding import PartitionSpec as P

FRAME = 64
MESH = pl.DeviceIdType.MESH


def gelu_parts(values):
    normal_cdf = 0.5 * (1.0 + lax.erf(values * 0.7071067811865476))
    density = jnp.exp(-0.5 * values * values) * 0.3989422804014327
    return (values * normal_cdf, normal_cdf + values * density)


def exchange_kernel(
    n, mp, inner, pieces,
    rows_ref, act_ref, place_ref, w_ref,
    rows_out, act_out, hid_out,
    terms_ref, parts, outbuf, w_buf, w_sem,
    rs_recv, rs_send, row_recv, row_send, act_recv, act_send, act_fwd, act_own,
    hid_recv, hid_send, local_sem,
):
    s = lax.axis_index("seq")
    m = lax.axis_index("mp")
    outer = n // inner
    z, xi = s // inner, s % inner
    stripe = rows_ref.shape[0]
    piece = stripe // pieces
    tokens = act_ref.shape[1]
    half = tokens // 2
    per = act_ref.shape[0]
    xfirst = inner == 2
    seq_peers = [((s + q) % n, m) for q in range(1, n)]
    mp_peers = [(s, (m + q) % mp) for q in range(1, mp)]

    opposite = (m + mp // 2) % mp
    greeted = seq_peers + mp_peers + [((s + q) % n, opposite) for q in range(1, n)]
    barrier = pltpu.get_barrier_semaphore()
    for peer in greeted:
        pl.semaphore_signal(barrier, inc=1, device_id=peer, device_id_type=MESH)
    pl.semaphore_wait(barrier, len(greeted))

    def remote(src, dst, send, recv, peer):
        return pltpu.make_async_remote_copy(
            src_ref=src, dst_ref=dst, send_sem=send, recv_sem=recv,
            device_id=peer, device_id_type=MESH,
        )

    def row_copy(t, p, way, peer, own=False):
        slot = rows_out.at[pl.ds(t * stripe + p * piece, piece)]
        src = rows_ref.at[pl.ds(p * piece, piece)] if own else slot
        return remote(src, slot, row_send.at[t, p, way], row_recv.at[t, p], peer)

    def go(run, copy):
        if run:
            copy.start()
        else:
            copy.wait_send()

    def arrive(run, t, p):
        if run:
            row_copy(t, p, 0, ((s + 1) % n, m)).wait_recv()

    def up(run, t, p, own=False):
        @pl.when(z < outer - 1)
        def _():
            go(run, row_copy(t, p, 0, (s + inner, m), own))

    def down(run, t, p, own=False):
        @pl.when(z > 0)
        def _():
            go(run, row_copy(t, p, 1, (s - inner, m), own))

    def across(run, t, p, own=False):
        for q in range(1, inner):
            go(run, row_copy(t, p, 1 + q, (z * inner + (xi + q) % inner, m), own))

    def loop(first, body):
        def step(p, carry):
            body(p)
            return carry
        lax.fori_loop(first, pieces, step, 0)

    def own_rows(run):
        def body(p):
            up(run, s, p, True)
            down(run, s, p, True)
            across(run, s, p, True)
        loop(0, body)

    def partner_rows(run):
        if xfirst:
            t = z * inner + (1 - xi)
            for p in range(2):
                arrive(run, t, p)
                up(run, t, p)
                down(run, t, p)

    def hop(run, d):
        def one(p, crossing):
            @pl.when(z >= d)
            def _():
                t = s - d * inner
                arrive(run, t, p)
                up(run, t, p)
                if crossing:
                    across(run, t, p)
                else:
                    t2 = (z - d) * inner + (1 - xi)
                    arrive(run, t2, p)
                    up(run, t2, p)

            @pl.when(z + d < outer)
            def _():
                t = s + d * inner
                arrive(run, t, p)
                down(run, t, p)
                if crossing:
                    across(run, t, p)
                else:
                    t2 = (z + d) * inner + (1 - xi)
                    arrive(run, t2, p)
                    down(run, t2, p)

        if xfirst:
            one(0, False)
            one(1, False)
            loop(2, lambda p: one(p, True))
        else:
            loop(0, lambda p: one(p, True))

    def rest_rows():
        for zz in range(outer):
            for q in range(1, inner):
                t = zz * inner + (xi + q) % inner
                loop(2 if xfirst else 0, lambda p: arrive(True, t, p))

    root_a = s // per
    root_b = (root_a + mp // 2) % mp

    def act_slot(t, h):
        return act_out.at[pl.ds(t * tokens + h * half, half)]

    def act_first(run):
        for j in range(per):
            target = m * per + j

            @pl.when(target != s)
            def _():
                for h, to in ((0, m), (1, opposite)):
                    go(run, remote(
                        act_ref.at[j, pl.ds(h * half, half)], act_slot(s, h),
                        act_send.at[j, h], act_recv.at[s, h], (target, to),
                    ))

            @pl.when(target == s)
            def _():
                for h in range(2):
                    for q, peer in enumerate(mp_peers):
                        go(run, remote(
                            act_ref.at[j, pl.ds(h * half, half)], act_slot(s, h),
                            act_own.at[h, q], act_recv.at[s, h], peer,
                        ))
                mine = pltpu.make_async_copy(
                    act_ref.at[j], act_out.at[pl.ds(s * tokens, tokens)], local_sem.at[1]
                )
                if run:
                    mine.start()
                else:
                    mine.wait()

    def act_wait(t, h):
        remote(act_slot(t, h), act_slot(t, h), act_fwd.at[0, 0], act_recv.at[t, h], mp_peers[0]).wait_recv()

    def act_pass(run):
        for h, root in ((0, root_a), (1, root_b)):
            @pl.when(m == root)
            def _():
                for k in range(1, n):
                    t = (s + k) % n
                    if run:
                        act_wait(t, h)
                    for q, peer in enumerate(mp_peers):
                        go(run, remote(
                            act_slot(t, h), act_slot(t, h), act_fwd.at[t, q], act_recv.at[t, h], peer,
                        ))

    def act_rest():
        for h, root in ((0, root_a), (1, root_b)):
            @pl.when(m != root)
            def _():
                for k in range(1, n):
                    act_wait((s + k) % n, h)

            @pl.when(m != root_a)
            def _():
                act_wait(s, h)

    def sums(run):
        for q, peer in enumerate(mp_peers):
            go(run, remote(terms_ref.at[peer[1]], parts.at[m], rs_send.at[q], rs_recv.at[m], peer))

    def hid_copy(q):
        peer = ((s + q) % n, m)
        return remote(
            outbuf.at[pl.ds(pl.multiple_of(peer[0] * FRAME, FRAME), FRAME)],
            hid_out.at[pl.ds(pl.multiple_of(s * FRAME, FRAME), FRAME)],
            hid_send.at[q], hid_recv.at[s], peer,
        )

    def hid_mine():
        at = pl.ds(pl.multiple_of(s * FRAME, FRAME), FRAME)
        return pltpu.make_async_copy(outbuf.at[at], hid_out.at[at], local_sem.at[2])

    def hidden():
        for q, peer in enumerate(mp_peers):
            remote(terms_ref.at[0], parts.at[peer[1]], rs_send.at[q], rs_recv.at[peer[1]], peer).wait_recv()
        width = parts.shape[2]
        chunk = 256 if width % 256 == 0 else width

        def step(c, carry):
            at = pl.ds(pl.multiple_of(c * chunk, chunk), chunk)
            total = terms_ref[m, :, at].astype(jnp.float32)
            for q in range(1, mp):
                total = total + parts[(m + q) % mp, :, at].astype(jnp.float32)
            outbuf[:, at] = jnp.dot(
                place_ref[...], total.astype(jnp.bfloat16), preferred_element_type=jnp.float32
            ).astype(jnp.bfloat16)
            return carry

        lax.fori_loop(0, width // chunk, step, 0)

    def hid_wait(t):
        at = pl.ds(pl.multiple_of(t * FRAME, FRAME), FRAME)
        remote(outbuf.at[pl.ds(0, FRAME)], hid_out.at[at], hid_send.at[1], hid_recv.at[t], seq_peers[0]).wait_recv()

    def multiply():
        width = terms_ref.shape[2]
        tile = w_buf.shape[1]
        per_part = width // tile

        def where(c):
            return (m + 1 + c // per_part) % mp, (c % per_part) * tile

        def fetch(c, slot):
            q, col = where(c)
            at = pl.ds(pl.multiple_of(q * width + col, tile), tile)
            return pltpu.make_async_copy(w_ref.at[at], w_buf.at[slot], w_sem.at[slot])

        count = mp * per_part
        fetch(0, 0).start()

        def step(c, carry):
            slot = c % 2

            @pl.when(c + 1 < count)
            def _():
                fetch(c + 1, 1 - slot).start()
            fetch(c, slot).wait()
            q, col = where(c)
            terms_ref[q, :, pl.ds(pl.multiple_of(col, tile), tile)] = lax.dot_general(
                rows_ref[...], w_buf[slot], (((1,), (1,)), ((), ())),
                preferred_element_type=jnp.float32,
            ).astype(jnp.bfloat16)
            return carry

        lax.fori_loop(0, count, step, 0)

    keep = pltpu.make_async_copy(rows_ref, rows_out.at[pl.ds(s * stripe, stripe)], local_sem.at[0])
    act_first(True)
    own_rows(True)
    keep.start()
    partner_rows(True)
    multiply()
    sums(True)
    hop(True, 1)
    act_pass(True)
    hidden()
    hop(True, 2)
    for q in range(1, n):
        hid_copy(q).start()
    hid_mine().start()
    for d in range(3, outer):
        hop(True, d)
    rest_rows()
    act_rest()
    for q in range(1, n):
        hid_wait((s + q) % n)

    keep.wait()
    hid_mine().wait()
    own_rows(False)
    sums(False)
    act_first(False)
    partner_rows(False)
    for d in range(1, outer):
        hop(False, d)
    act_pass(False)
    for q in range(1, n):
        hid_copy(q).wait_send()


def exchange(n, mp, tag, rows, acts, place, w_out):
    stripe, quarter = rows.shape
    per, tokens, kept = acts.shape
    width = w_out.shape[0] // mp
    inner = n // 4
    pieces = stripe // 32 if inner == 2 else 1
    vm = pl.BlockSpec(memory_space=pltpu.VMEM)
    anywhere = pl.BlockSpec(memory_space=pl.ANY)
    dma = pltpu.SemaphoreType.DMA
    return pl.pallas_call(
        functools.partial(exchange_kernel, n, mp, inner, pieces),
        out_shape=(
            jax.ShapeDtypeStruct((n * stripe, quarter), jnp.bfloat16),
            jax.ShapeDtypeStruct((n * tokens, kept), jnp.bfloat16),
            jax.ShapeDtypeStruct((n * FRAME, width), jnp.bfloat16),
        ),
        in_specs=[vm] * 3 + [anywhere],
        out_specs=(anywhere,) * 3,
        scratch_shapes=[
            pltpu.VMEM((mp, stripe, width), jnp.bfloat16),
            pltpu.VMEM((mp, stripe, width), jnp.bfloat16),
            pltpu.VMEM((n * FRAME, width), jnp.bfloat16),
            pltpu.VMEM((2, 256 if width % 256 == 0 else width, quarter), jnp.bfloat16),
            dma((2,)),
            dma((mp,)), dma((mp,)),
            dma((n, pieces)), dma((n, pieces, 1 + inner)),
            dma((n, 2)), dma((per, 2)), dma((n, mp)), dma((2, mp)),
            dma((n,)), dma((n,)), dma((3,)),
        ],
        compiler_params=pltpu.CompilerParams(
            collective_id=tag, has_side_effects=True, vmem_limit_bytes=60 * 1024 * 1024
        ),
    )(rows, acts, place, w_out)


def spread(counts, before, base, size):
    r = jnp.arange(size, dtype=jnp.int32)
    inside = (r >= before[..., None]) & (r < (before + counts)[..., None])
    return jnp.sum(jnp.where(inside, (base - before)[..., None] + r + 1, 0), axis=-2) - 1


def local(n, mp, grad_rows, img_start, img_len, img_owner, pre_act, w_out):
    stripe, quarter = grad_rows.shape
    width = pre_act.shape[1]
    kept = w_out.shape[0] // n
    frames = stripe // FRAME
    here = lax.axis_index("seq")
    owner = img_owner.reshape(n, frames)
    starts = img_start.reshape(n, frames)
    lengths = img_len.reshape(n, frames)
    before = jnp.cumsum(lengths, axis=1) - lengths
    row = jnp.arange(FRAME, dtype=jnp.int32)
    column = jnp.arange(stripe, dtype=jnp.int32)

    values = pre_act.astype(jnp.float32)
    activation, derivative = gelu_parts(values)
    activation = activation.astype(jnp.bfloat16)
    acts = activation.reshape(stripe, width // kept, kept).transpose(1, 0, 2)

    my_owner = lax.dynamic_slice_in_dim(owner, here, 1)[0]
    my_start = lax.dynamic_slice_in_dim(starts, here, 1)[0] - here * stripe
    my_length = lax.dynamic_slice_in_dim(lengths, here, 1)[0]
    my_before = lax.dynamic_slice_in_dim(before, here, 1)[0]
    to = (my_owner[None, :] == jnp.arange(n, dtype=jnp.int32)[:, None]).astype(jnp.int32)
    first = jnp.sum(to * my_before[None, :], axis=1)
    count = jnp.sum(to * my_length[None, :], axis=1)
    at = jnp.where(row[None, :] < count[:, None], first[:, None] + row[None, :], -1).reshape(n * FRAME, 1)
    order = img_owner * frames + jnp.arange(n * frames, dtype=jnp.int32) % frames
    factor = 1.0 / math.sqrt(n * stripe)

    def with_size(tag, size, grad_rows, acts, w_out):
        source = spread(my_length, my_before, my_start, size)
        live = (source[:, None] == column[None, :]).astype(jnp.bfloat16)
        rows = jnp.dot(live, grad_rows, preferred_element_type=jnp.float32).astype(jnp.bfloat16)
        place = (at == jnp.arange(size, dtype=jnp.int32)[None, :]).astype(jnp.bfloat16)
        rows_all, act_all, hid = exchange(n, mp, tag, rows, acts, place, w_out)
        blocks = act_all.reshape(n * frames, FRAME, kept)[order].reshape(n, stripe, kept)
        block = jnp.broadcast_to(jnp.arange(frames, dtype=jnp.int32) * FRAME, (n, frames))
        taken = spread(lengths, before, block, size)
        lined = (taken[:, :, None] == column[None, None, :]).astype(jnp.bfloat16)
        act_rows = jnp.einsum(
            "trc,tck->trk", lined, blocks, preferred_element_type=jnp.float32
        ).astype(jnp.bfloat16).reshape(n * size, kept)
        product = lax.dot_general(
            act_rows, rows_all, (((0,), (0,)), ((), ())), preferred_element_type=jnp.float32
        ) * factor
        return lax.optimization_barrier(product.astype(jnp.bfloat16)), hid

    sizes = [stripe // 16 * k for k in (12, 13, 16)]
    most = jnp.max(jnp.sum(lengths, axis=1))
    which = sum((most > size).astype(jnp.int32) for size in sizes[:-1])
    weight_grad, hid = lax.switch(
        which,
        [functools.partial(with_size, tag, size) for tag, size in enumerate(sizes)],
        grad_rows, acts, w_out,
    )

    came = jnp.arange(n * FRAME, dtype=jnp.int32)
    from_me = (owner == here).T
    pick = jnp.repeat(jnp.repeat(from_me, FRAME, axis=0), FRAME, axis=1)
    pick = (pick & (column[:, None] % FRAME == came[None, :] % FRAME)).astype(jnp.bfloat16)
    hidden_grad = jnp.dot(pick, hid, preferred_element_type=jnp.float32)
    pre_grad = (hidden_grad * derivative).astype(jnp.bfloat16)
    return (pre_grad, weight_grad)


def fused_kernel(
    n, mp, inner, pieces, early, factor,
    order_ref, rows_ref, act_ref, place_ref, taken_ref, w_ref,
    hid_out, grad_out,
    rows_all, act_all, w_all, acc, hot, block, lined, picked, terms, parts, hid, stage,
    w_sem, rs_recv, rs_send, row_recv, row_send, act_recv, act_send, act_fwd, act_own,
    local_sem, out_sem,
):
    s = lax.axis_index("seq")
    m = lax.axis_index("mp")
    outer = n // inner
    z, xi = s // inner, s % inner
    size = rows_ref.shape[0]
    piece = size // pieces
    per, frames, _, kept = act_ref.shape
    half = frames // 2
    quarter = rows_ref.shape[1]
    width = parts.shape[3]
    seq_peers = [((s + q) % n, m) for q in range(1, n)]
    mp_peers = [(s, (m + q) % mp) for q in range(1, mp)]
    opposite = (m + mp // 2) % mp
    greeted = seq_peers + mp_peers + [((s + q) % n, opposite) for q in range(1, n)]
    barrier = pltpu.get_barrier_semaphore()
    for peer in greeted:
        pl.semaphore_signal(barrier, inc=1, device_id=peer, device_id_type=MESH)
    pl.semaphore_wait(barrier, len(greeted))

    def remote(src, dst, send, recv, peer):
        return pltpu.make_async_remote_copy(
            src_ref=src, dst_ref=dst, send_sem=send, recv_sem=recv,
            device_id=peer, device_id_type=MESH,
        )

    def row_copy(t, p, way, peer, own=False):
        slot = rows_all.at[t, pl.ds(p * piece, piece)]
        src = rows_ref.at[pl.ds(p * piece, piece)] if own else slot
        return remote(src, slot, row_send.at[t, p, way], row_recv.at[t, p], peer)

    def go(run, copy):
        if run:
            copy.start()
        else:
            copy.wait_send()

    def arrive(run, t, p):
        if run:
            row_copy(t, p, 0, ((s + 1) % n, m)).wait_recv()

    def up(run, t, p, own=False):
        @pl.when(z < outer - 1)
        def _():
            go(run, row_copy(t, p, 0, (s + inner, m), own))

    def down(run, t, p, own=False):
        @pl.when(z > 0)
        def _():
            go(run, row_copy(t, p, 1, (s - inner, m), own))

    def across(run, t, p, own=False):
        go(run, row_copy(t, p, 2, (z * inner + 1 - xi, m), own))

    def loop(first, last, body):
        def step(p, carry):
            body(p)
            return carry
        lax.fori_loop(first, last, step, 0)

    def own_rows(run):
        def body(p):
            up(run, s, p, True)
            down(run, s, p, True)
            across(run, s, p, True)
        loop(0, pieces, body)

    def partner_rows(run):
        t = z * inner + (1 - xi)
        for p in range(early):
            arrive(run, t, p)
            up(run, t, p)
            down(run, t, p)

    def hop(run, d, first, last):
        def one(p, crossing):
            @pl.when(z >= d)
            def _():
                t = s - d * inner
                arrive(run, t, p)
                up(run, t, p)
                if crossing:
                    across(run, t, p)
                else:
                    t2 = (z - d) * inner + (1 - xi)
                    arrive(run, t2, p)
                    up(run, t2, p)

            @pl.when(z + d < outer)
            def _():
                t = s + d * inner
                arrive(run, t, p)
                down(run, t, p)
                if crossing:
                    across(run, t, p)
                else:
                    t2 = (z + d) * inner + (1 - xi)
                    arrive(run, t2, p)
                    down(run, t2, p)

        for p in range(first, min(last, early)):
            one(p, False)
        loop(max(first, early), last, lambda p: one(p, True))

    def rest(layer):
        t = layer * inner + (1 - xi)
        loop(early, pieces, lambda p: arrive(True, t, p))

    root_a = s // per
    root_b = (root_a + mp // 2) % mp

    def act_slot(t, h):
        return act_all.at[pl.ds(t * frames + h * half, half)]

    def act_piece(j, h):
        return act_ref.at[j, pl.ds(h * half, half)]

    def act_mine(j):
        return pltpu.make_async_copy(
            act_ref.at[j], act_all.at[pl.ds(s * frames, frames)], local_sem.at[1]
        )

    def act_first(run):
        for j in range(per):
            target = m * per + j

            @pl.when(target != s)
            def _():
                for h, to in ((0, m), (1, opposite)):
                    go(run, remote(
                        act_piece(j, h), act_slot(s, h),
                        act_send.at[j, h], act_recv.at[s, h], (target, to),
                    ))

            @pl.when(target == s)
            def _():
                for h in range(2):
                    for q, peer in enumerate(mp_peers):
                        go(run, remote(
                            act_piece(j, h), act_slot(s, h),
                            act_own.at[h, q], act_recv.at[s, h], peer,
                        ))
                if run:
                    act_mine(j).start()

    def act_wait(t, h):
        remote(act_slot(t, h), act_slot(t, h), act_fwd.at[0, 0], act_recv.at[t, h], mp_peers[0]).wait_recv()

    def act_pass(run):
        for h, root in ((0, root_a), (1, root_b)):
            @pl.when(m == root)
            def _():
                for k in range(1, n):
                    t = (s + k) % n
                    if run:
                        act_wait(t, h)
                    for q, peer in enumerate(mp_peers):
                        go(run, remote(
                            act_slot(t, h), act_slot(t, h), act_fwd.at[t, q], act_recv.at[t, h], peer,
                        ))

    def act_rest():
        for h, root in ((0, root_a), (1, root_b)):
            @pl.when(m != root)
            def _():
                for k in range(1, n):
                    act_wait((s + k) % n, h)

            @pl.when(m != root_a)
            def _():
                act_wait(s, h)

        @pl.when(m == root_a)
        def _():
            act_mine(s % per).wait()

    def layer_of(k):
        if k == 0:
            return z
        low = outer // 2
        if k == 1:
            return jnp.where(z < low, low - 1 - z, 3 * low - 1 - z)
        return jnp.where(z < low, k, outer - 1 - k)

    def sums(run, g):
        for q, peer in enumerate(mp_peers):
            part_copy(run, g, q, peer)

    def part_copy(run, g, q, peer):
        go(run, remote(
            terms.at[peer[1]], parts.at[g, m], rs_send.at[g, q], rs_recv.at[g, m], peer,
        ))

    def select(layer):
        tile = 512 if quarter % 512 == 0 else quarter
        for j in range(inner):
            t = layer * inner + j

            def step(c):
                at = pl.ds(pl.multiple_of(c * tile, tile), tile)
                picked[pl.ds(j * FRAME, FRAME), at] = jnp.dot(
                    place_ref[pl.ds(pl.multiple_of(t * FRAME, FRAME), FRAME), :],
                    rows_all[t, :, at], preferred_element_type=jnp.float32,
                ).astype(jnp.bfloat16)
            loop(0, quarter // tile, step)

    def hidden(g, layer):
        select(layer)
        if g > 0:
            sums(False, g - 1)
        tile = 256 if width % 256 == 0 else width
        for q in range(mp):
            to = (m + 1 + q) % mp

            def step(c):
                col = pl.multiple_of(c * tile, tile)
                value = lax.dot_general(
                    picked[...], w_all[pl.ds(pl.multiple_of(to * width + c * tile, tile), tile), :],
                    (((1,), (1,)), ((), ())), preferred_element_type=jnp.float32,
                ).astype(jnp.bfloat16)
                if q < mp - 1:
                    terms[to, :, pl.ds(col, tile)] = value
                else:
                    parts[g, m, :, pl.ds(col, tile)] = value
            loop(0, width // tile, step)
            if q > 0:
                part_copy(True, g, q - 1, mp_peers[q - 1])

    def reduce(g, layer):
        for q, peer in enumerate(mp_peers):
            remote(
                terms.at[0], parts.at[g, peer[1]], rs_send.at[g, q], rs_recv.at[g, peer[1]], peer
            ).wait_recv()
        tile = 256 if width % 256 == 0 else width
        for j in range(inner):
            t = layer * inner + j

            def step(c):
                at = pl.ds(pl.multiple_of(c * tile, tile), tile)
                rows = pl.ds(j * FRAME, FRAME)
                total = parts[g, 0, rows, at].astype(jnp.float32)
                for q in range(1, mp):
                    total = total + parts[g, q, rows, at].astype(jnp.float32)
                hid[t, :, at] = total.astype(jnp.bfloat16)
            loop(0, width // tile, step)

    def line_up(layer):
        for j in range(inner):
            t = layer * inner + j

            def frame(f):
                at = pl.ds(pl.multiple_of(f * FRAME, FRAME), FRAME)
                block[at, :] = act_all[order_ref[t * frames + f]]
                row = lax.broadcasted_iota(jnp.int32, (FRAME, size), 0) + f * FRAME
                hot[at, :] = jnp.where(row == taken_ref[t], 1.0, 0.0).astype(jnp.bfloat16)
            loop(0, frames, frame)

            def step(c):
                at = pl.ds(pl.multiple_of(c * 128, 128), 128)
                lined[j, at, :] = lax.dot_general(
                    block[:, at], hot[...], (((0,), (0,)), ((), ())),
                    preferred_element_type=jnp.float32,
                ).astype(jnp.bfloat16)
            loop(0, kept // 128, step)

    def weights(g, layer, last):
        line_up(layer)
        tile = 256 if quarter % 256 == 0 else quarter
        count = quarter // tile

        def put(c, slot):
            at = pl.ds(pl.multiple_of(c * tile, tile), tile)
            return pltpu.make_async_copy(stage.at[slot], grad_out.at[:, at], out_sem.at[slot])

        def step(c):
            at = pl.ds(pl.multiple_of(c * tile, tile), tile)
            value = jnp.dot(lined[0], rows_all[layer * inner, :, at], preferred_element_type=jnp.float32)
            for j in range(1, inner):
                value = value + jnp.dot(
                    lined[j], rows_all[layer * inner + j, :, at], preferred_element_type=jnp.float32
                )
            if g > 0:
                value = value + acc[:, at]
            if not last:
                acc[:, at] = value
                return
            slot = c % 2

            @pl.when(c > 1)
            def _():
                put(c - 2, slot).wait()
            stage[slot] = (value * factor).astype(jnp.bfloat16)
            put(c, slot).start()
        loop(0, count, step)
        if last:
            for c in range(max(0, count - 2), count):
                put(c, c % 2).wait()

    fetch = pltpu.make_async_copy(w_ref, w_all, w_sem)
    keep = pltpu.make_async_copy(rows_ref, rows_all.at[s], local_sem.at[0])
    act_first(True)
    own_rows(True)
    keep.start()
    fetch.start()
    partner_rows(True)
    act_pass(True)
    hop(True, 1, 0, pieces)
    keep.wait()
    fetch.wait()
    rest(layer_of(0))
    hidden(0, layer_of(0))
    rest(layer_of(1))
    act_rest()
    weights(0, layer_of(0), False)
    reduce(0, layer_of(0))
    hidden(1, layer_of(1))
    weights(1, layer_of(1), False)
    hop(True, 2, 0, pieces)
    rest(layer_of(2))
    reduce(1, layer_of(1))
    hidden(2, layer_of(2))
    weights(2, layer_of(2), False)
    hop(True, 3, 0, pieces)
    rest(layer_of(3))
    reduce(2, layer_of(2))
    hidden(3, layer_of(3))
    weights(3, layer_of(3), True)
    reduce(3, layer_of(3))
    for f in range(frames):
        hid_out[pl.ds(f * FRAME, FRAME), :] = hid[order_ref[n * frames + f]]

    act_first(False)
    own_rows(False)
    sums(False, outer - 1)
    partner_rows(False)
    for d in range(1, outer):
        hop(False, d, 0, pieces)
    act_pass(False)


def fused(n, mp, tag, factor, order, rows, acts, place, taken, w_out):
    stripe, quarter = rows.shape
    per, frames, _, kept = acts.shape
    width = w_out.shape[0] // mp
    inner = n // 4
    outer = n // inner
    pieces = stripe // 32
    vm = pl.BlockSpec(memory_space=pltpu.VMEM)
    anywhere = pl.BlockSpec(memory_space=pl.ANY)
    dma = pltpu.SemaphoreType.DMA
    b16 = jnp.bfloat16
    return pl.pallas_call(
        functools.partial(fused_kernel, n, mp, inner, pieces, 1, factor),
        out_shape=(
            jax.ShapeDtypeStruct((frames * FRAME, width), b16),
            jax.ShapeDtypeStruct((kept, quarter), b16),
        ),
        in_specs=[pl.BlockSpec(memory_space=pltpu.SMEM)] + [vm] * 4 + [anywhere],
        out_specs=(vm, anywhere),
        scratch_shapes=[
            pltpu.VMEM((n, stripe, quarter), b16),
            pltpu.VMEM((n * frames, FRAME, kept), b16),
            pltpu.VMEM(w_out.shape, b16),
            pltpu.VMEM((kept, quarter), jnp.float32),
            pltpu.VMEM((frames * FRAME, stripe), b16),
            pltpu.VMEM((frames * FRAME, kept), b16),
            pltpu.VMEM((inner, kept, stripe), b16),
            pltpu.VMEM((inner * FRAME, quarter), b16),
            pltpu.VMEM((mp, inner * FRAME, width), b16),
            pltpu.VMEM((outer, mp, inner * FRAME, width), b16),
            pltpu.VMEM((n, FRAME, width), b16),
            pltpu.VMEM((2, kept, 256 if quarter % 256 == 0 else quarter), b16),
            dma(()), dma((outer, mp)), dma((outer, mp)),
            dma((n, pieces)), dma((n, pieces, 3)),
            dma((n, 2)), dma((per, 2)), dma((n, mp)), dma((2, mp)),
            dma((2,)), dma((2,)),
        ],
        compiler_params=pltpu.CompilerParams(
            collective_id=tag, has_side_effects=True, vmem_limit_bytes=67043328
        ),
    )(order, rows, acts, place, taken, w_out)


def local_fused(n, mp, grad_rows, img_start, img_len, img_owner, pre_act, w_out):
    stripe, quarter = grad_rows.shape
    width = pre_act.shape[1]
    kept = w_out.shape[0] // n
    frames = stripe // FRAME
    per = width // kept
    here = lax.axis_index("seq")
    owner = img_owner.reshape(n, frames)
    starts = img_start.reshape(n, frames)
    lengths = img_len.reshape(n, frames)
    before = jnp.cumsum(lengths, axis=1) - lengths
    row = jnp.arange(FRAME, dtype=jnp.int32)
    column = jnp.arange(stripe, dtype=jnp.int32)

    values = pre_act.astype(jnp.float32)
    activation, derivative = gelu_parts(values)
    activation = activation.astype(jnp.bfloat16)
    acts = activation.reshape(stripe, per, kept).transpose(1, 0, 2).reshape(per, frames, FRAME, kept)

    my_start = lax.dynamic_slice_in_dim(starts, here, 1)[0] - here * stripe
    my_length = lax.dynamic_slice_in_dim(lengths, here, 1)[0]
    my_before = lax.dynamic_slice_in_dim(before, here, 1)[0]
    mine = (owner == here).astype(jnp.int32)
    first = jnp.sum(mine * before, axis=1)
    count = jnp.sum(mine * lengths, axis=1)
    at = jnp.where(row[None, :] < count[:, None], first[:, None] + row[None, :], -1).reshape(n * FRAME, 1)
    source_of = jnp.sum(mine * jnp.arange(n, dtype=jnp.int32)[:, None], axis=0)
    order = img_owner * frames + jnp.arange(n * frames, dtype=jnp.int32) % frames
    order = jnp.concatenate([order, source_of])
    factor = 1.0 / math.sqrt(n * stripe)
    block = jnp.broadcast_to(jnp.arange(frames, dtype=jnp.int32) * FRAME, (n, frames))

    def with_size(tag, size, grad_rows, acts, w_out):
        source = spread(my_length, my_before, my_start, size)
        live = (source[:, None] == column[None, :]).astype(jnp.bfloat16)
        rows = jnp.dot(live, grad_rows, preferred_element_type=jnp.float32).astype(jnp.bfloat16)
        place = (at == jnp.arange(size, dtype=jnp.int32)[None, :]).astype(jnp.bfloat16)
        taken = spread(lengths, before, block, size).reshape(n, 1, size)
        return fused(n, mp, tag, factor, order, rows, acts, place, taken, w_out)

    sizes = [stripe // 16 * k for k in (12, 13, 16)]
    most = jnp.max(jnp.sum(lengths, axis=1))
    which = sum((most > size).astype(jnp.int32) for size in sizes[:-1])
    hid, weight_grad = lax.switch(
        which,
        [functools.partial(with_size, tag, size) for tag, size in enumerate(sizes)],
        grad_rows, acts, w_out,
    )
    pre_grad = (hid.astype(jnp.float32) * derivative).astype(jnp.bfloat16)
    return (pre_grad, weight_grad)


def chosen(n, mp, grad_rows, *rest):
    whole = n * grad_rows.shape[0] * grad_rows.shape[1] + rest[-1].shape[0] * rest[-1].shape[1]
    fits = n * FRAME == grad_rows.shape[0] and 2 * whole <= 40 * 1024 * 1024
    return (local_fused if fits else local)(n, mp, grad_rows, *rest)


def solution(mesh):
    return jax.shard_map(
        functools.partial(chosen, mesh.shape["seq"], mesh.shape["mp"]),
        mesh=mesh,
        in_specs=(P("seq", "mp"), P(), P(), P(), P("seq", "mp"), P(None, "mp")),
        out_specs=(P("seq", "mp"), P("seq", "mp")),
        check_vma=False,
    )
```

profile of v0, /device:TPU:0, one launch (start us, length us, event | category | flops | bytes accessed | tf_op | source)
XLA Modules:
  0.0 285.6 jit_solution(2420594064310418973)
XLA Ops:
  0.6 0.7 fusion.27
  1.3 0.7 broadcast_compare_fusion
  2.0 0.1 eq.118
  2.1 0.6 pad_add_fusion
  2.7 0.7 reshape.144
  3.4 0.2 reduce_window_sum.11
  3.6 0.1 fusion.28
  3.7 0.6 reduce_max.9
  5.7 0.1 lt.147
  5.8 0.0 copy-start.1
  5.8 0.0 copy-start.2
  5.8 2.1 fusion.21
  7.8 1.2 copy.12
  9.0 0.0 copy-done.1
  9.0 0.0 copy-done.2
  9.0 271.3 %conditional.2 = (bf16[640,2048]{1,0:T(8,128)(2,1)}, bf16[512,1280]{1,0:T(8,128)(2,1)}) conditional(s32[]{:T(128)} %clamp.3, (s32[1,8]{1,0:T(1,128)S(1)}, s32[8,8]{1,0:T(8,128)S(1)}, s32[]{:T(128)}, s32[64]{0:T(128)S(1)}, s32[]{:T(128)}, /*index=5*/s32[512]{0:T(512)S(1)}, bf16[512,2048]{1,0:T(8,128)(2,1)S(1)}, ...), branch_computations={%region_4.9_spmd, %region_9.14_spmd, %region_14.19_spmd} | conditional | flops 1075836800 | bytes 4838212
  9.0 0.1 reshape.136
  9.1 0.1 select_reduce_fusion.1
  9.2 0.1 select_reduce_fusion.2
  9.4 0.1 add.203
  9.4 0.1 add.204
  9.5 0.1 lt.112
  9.6 0.1 lt.113
  9.7 0.1 select_reduce_fusion
  9.8 0.6 sub.71.taken_ref
  10.4 0.9 fusion.place_ref
  11.3 2.2 convolution_convert_fusion.rows_ref
  13.5 257.0 %branch_0_fun.2 = (bf16[512,1280]{1,0:T(8,128)(2,1)}, bf16[640,2048]{1,0:T(8,128)(2,1)}) custom-call(s32[72]{0:T(128)} %get-tuple-element.358.order_ref, bf16[384,2048]{1,0:T(8,128)(2,1)} %convolution_convert_fusion.rows_ref, bf16[2,8,64,640]{3,2,1,0:T(8,128)(2,1)} %bitcast.3.act_ref, bf16[512,384]{1,0:T(8,128)(2,1)} %fusion.place_ref, ...), custom_call_target="tpu_custom_call" | custom-call | tf_op jit(solution)/shard_map/cond/branch_0_fun/pallas_call | solution.py:773
  280.3 0.0 copy-start
  280.3 3.5 %fusion.26 = bf16[512,1280]{1,0:T(8,128)(2,1)} fusion(bf16[512,1280]{1,0:T(8,128)(2,1)} %param.13, bf16[512,1280]{1,0:T(8,128)(2,1)} %get-tuple-element.413), kind=kLoop, calls=%fused_computation.82 | loop fusion | flops 7864320 | bytes 3932160 | tf_op jit(solution)/shard_map/convert_element_type | solution.py:853
  283.9 0.0 copy-done
  283.9 1.5 copy.20
  (10 shorter events, 0.1 us)
Async XLA Ops:
  5.8 3.3 %copy-start.1 = (s32[64]{0:T(128)S(1)}, s32[64]{0:T(128)}, u32[]{:S(2)}) copy-start(s32[64]{0:T(128)} %param.10) | copy-start | bytes 772
  5.8 3.3 %copy-start.2 = (bf16[512,2048]{1,0:T(8,128)(2,1)S(1)}, bf16[512,2048]{1,0:T(8,128)(2,1)}, u32[]{:S(2)}) copy-start(bf16[512,2048]{1,0:T(8,128)(2,1)} %param.9) | copy-start | bytes 6291460
  280.3 3.5 %copy-start = (bf16[640,2048]{1,0:T(8,128)(2,1)S(1)}, bf16[640,2048]{1,0:T(8,128)(2,1)}, u32[]{:S(2)}) copy-start(bf16[640,2048]{1,0:T(8,128)(2,1)} %get-tuple-element.444) | copy-start | bytes 7864324
where the time goes:
time: 289 us; the launch traced here: 286 us
  Pallas kernels  257 us (89%)
  loops' own time  9.81 us (3%)
  other arithmetic  9.76 us (3%)
  local copies, waits for them, and re-layouts  4.57 us (2%)
    pallas_call x1, Pallas kernels, fused(): pl.pallas_call(functools.partial(fused_kernel, n, mp, inner, pieces, 1, f...  257 us
    unnamed x1, loops' own time  9.81 us

commit v1 on v0

--- a/solution.py
+++ b/solution.py
@@ -416,24 +416,28 @@
     n, mp, inner, pieces, early, factor,
     order_ref, rows_ref, act_ref, place_ref, taken_ref, w_ref,
     hid_out, grad_out,
-    rows_all, act_all, w_all, acc, hot, block, lined, picked, terms, parts, hid, stage,
+    rows_all, act_all, relay, w_all, acc, hot, block, lined, picked, terms, parts, hid, stage,
     w_sem, rs_recv, rs_send, row_recv, row_send, act_recv, act_send, act_fwd, act_own,
-    local_sem, out_sem,
+    relay_recv, relay_send, relay_fwd, far_recv, far_send, local_sem, out_sem,
 ):
     s = lax.axis_index("seq")
     m = lax.axis_index("mp")
     outer = n // inner
+    low = outer // 2
     z, xi = s // inner, s % inner
     size = rows_ref.shape[0]
     piece = size // pieces
     per, frames, _, kept = act_ref.shape
     half = frames // 2
     quarter = rows_ref.shape[1]
-    width = parts.shape[3]
+    width = parts.shape[1]
+    pair = inner * FRAME
+    edge = (z == 0) | (z == outer - 1)
+    sibling = m + 1 - 2 * (m % 2)
+    opposite = (m + mp // 2) % mp
     seq_peers = [((s + q) % n, m) for q in range(1, n)]
     mp_peers = [(s, (m + q) % mp) for q in range(1, mp)]
-    opposite = (m + mp // 2) % mp
-    greeted = seq_peers + mp_peers + [((s + q) % n, opposite) for q in range(1, n)]
+    greeted = seq_peers + mp_peers
     barrier = pltpu.get_barrier_semaphore()
     for peer in greeted:
         pl.semaphore_signal(barrier, inc=1, device_id=peer, device_id_type=MESH)
@@ -445,64 +449,75 @@
             device_id=peer, device_id_type=MESH,
         )
 
-    def row_copy(t, p, way, peer, own=False):
-        slot = rows_all.at[t, pl.ds(p * piece, piece)]
-        src = rows_ref.at[pl.ds(p * piece, piece)] if own else slot
-        return remote(src, slot, row_send.at[t, p, way], row_recv.at[t, p], peer)
-
     def go(run, copy):
         if run:
             copy.start()
         else:
             copy.wait_send()
 
-    def arrive(run, t, p):
-        if run:
-            row_copy(t, p, 0, ((s + 1) % n, m)).wait_recv()
-
-    def up(run, t, p, own=False):
-        @pl.when(z < outer - 1)
-        def _():
-            go(run, row_copy(t, p, 0, (s + inner, m), own))
-
-    def down(run, t, p, own=False):
-        @pl.when(z > 0)
-        def _():
-            go(run, row_copy(t, p, 1, (s - inner, m), own))
-
-    def across(run, t, p, own=False):
-        go(run, row_copy(t, p, 2, (z * inner + 1 - xi, m), own))
-
     def loop(first, last, body):
         def step(p, carry):
             body(p)
             return carry
         lax.fori_loop(first, last, step, 0)
 
-    def own_rows(run):
+    def layer_of(k):
+        mate = jnp.where(z < low, low - 1 - z, 3 * low - 1 - z)
+        return jnp.where(k == 0, z, jnp.where(k == 1, mate, jnp.where(z < low, k, outer - 1 - k)))
+
+    def row_copy(t, p, way, peer, own=False):
+        slot = rows_all.at[t // inner, pl.ds((t % inner) * size + p * piece, piece)]
+        src = rows_ref.at[pl.ds(p * piece, piece)] if own else slot
+        return remote(src, slot, row_send.at[t, p, way], row_recv.at[t, p], peer)
+
+    def arrive(run, t, p):
+        if run:
+            row_copy(t, p, 0, ((s + 1) % n, m)).wait_recv()
+
+    def up(run, t, p, own=False):
+        @pl.when(z < outer - 1)
+        def _():
+            go(run, row_copy(t, p, 0, (s + inner, m), own))
+
+    def down(run, t, p, own=False):
+        @pl.when(z > 0)
+        def _():
+            go(run, row_copy(t, p, 1, (s - inner, m), own))
+
+    def across(run, t, p, own=False):
+        go(run, row_copy(t, p, 2, (z * inner + 1 - xi, m), own))
+
+    def own_rows(run, first, last):
         def body(p):
             up(run, s, p, True)
             down(run, s, p, True)
             across(run, s, p, True)
-        loop(0, pieces, body)
-
-    def partner_rows(run):
+        loop(first, last, body)
+
+    def partner_row(run, p):
         t = z * inner + (1 - xi)
-        for p in range(early):
-            arrive(run, t, p)
-            up(run, t, p)
-            down(run, t, p)
+        arrive(run, t, p)
+        up(run, t, p)
+        down(run, t, p)
 
     def hop(run, d, first, last):
-        def one(p, crossing):
+        def one(p):
+            @pl.when(edge & (d == 1) & (p >= early))
+            def _():
+                partner_row(run, p)
+
             @pl.when(z >= d)
             def _():
                 t = s - d * inner
                 arrive(run, t, p)
                 up(run, t, p)
-                if crossing:
+
+                @pl.when((p >= early) & ((d > 1) | (z > 1)))
+                def _():
                     across(run, t, p)
-                else:
+
+                @pl.when(p < early)
+                def _():
                     t2 = (z - d) * inner + (1 - xi)
                     arrive(run, t2, p)
                     up(run, t2, p)
@@ -512,20 +527,24 @@
                 t = s + d * inner
                 arrive(run, t, p)
                 down(run, t, p)
-                if crossing:
+
+                @pl.when((p >= early) & ((d > 1) | (z < outer - 2)))
+                def _():
                     across(run, t, p)
-                else:
+
+                @pl.when(p < early)
+                def _():
                     t2 = (z + d) * inner + (1 - xi)
                     arrive(run, t2, p)
                     down(run, t2, p)
-
-        for p in range(first, min(last, early)):
-            one(p, False)
-        loop(max(first, early), last, lambda p: one(p, True))
-
-    def rest(layer):
-        t = layer * inner + (1 - xi)
-        loop(early, pieces, lambda p: arrive(True, t, p))
+        loop(first, last, one)
+
+    def rest(k):
+        t = layer_of(k) * inner + (1 - xi)
+
+        @pl.when((k > 0) | jnp.logical_not(edge))
+        def _():
+            loop(early, pieces, lambda p: arrive(True, t, p))
 
     root_a = s // per
     root_b = (root_a + mp // 2) % mp
@@ -536,9 +555,9 @@
     def act_piece(j, h):
         return act_ref.at[j, pl.ds(h * half, half)]
 
-    def act_mine(j):
+    def act_mine():
         return pltpu.make_async_copy(
-            act_ref.at[j], act_all.at[pl.ds(s * frames, frames)], local_sem.at[1]
+            act_ref.at[xi], act_all.at[pl.ds(s * frames, frames)], local_sem.at[1]
         )
 
     def act_first(run):
@@ -547,125 +566,175 @@
 
             @pl.when(target != s)
             def _():
-                for h, to in ((0, m), (1, opposite)):
-                    go(run, remote(
-                        act_piece(j, h), act_slot(s, h),
-                        act_send.at[j, h], act_recv.at[s, h], (target, to),
-                    ))
+                go(run, remote(
+                    act_piece(j, 1), relay.at[j], relay_send.at[j], relay_recv.at[j], (s, opposite)
+                ))
+                go(run, remote(
+                    act_piece(j, 0), act_slot(s, 0), act_send.at[j], act_recv.at[s, 0], (target, m)
+                ))
 
             @pl.when(target == s)
             def _():
                 for h in range(2):
-                    for q, peer in enumerate(mp_peers):
+                    for q, to in enumerate((opposite, sibling)):
                         go(run, remote(
-                            act_piece(j, h), act_slot(s, h),
-                            act_own.at[h, q], act_recv.at[s, h], peer,
+                            act_piece(j, h), act_slot(s, h), act_own.at[h, q], act_recv.at[s, h], (s, to)
                         ))
                 if run:
-                    act_mine(j).start()
+                    act_mine().start()
+
+    def act_relay(run):
+        for j in range(per):
+            target = opposite * per + j
+
+            @pl.when(target != s)
+            def _():
+                if run:
+                    remote(
+                        relay.at[j], relay.at[j], relay_send.at[j], relay_recv.at[j], (s, opposite)
+                    ).wait_recv()
+                go(run, remote(
+                    relay.at[j], act_slot(s, 1), relay_fwd.at[j], act_recv.at[s, 1], (target, m)
+                ))
 
     def act_wait(t, h):
-        remote(act_slot(t, h), act_slot(t, h), act_fwd.at[0, 0], act_recv.at[t, h], mp_peers[0]).wait_recv()
+        remote(act_slot(t, h), act_slot(t, h), act_fwd.at[0, 0, 0], act_recv.at[t, h], mp_peers[0]).wait_recv()
+
+    def act_send_on(run, t, h, to, q):
+        go(run, remote(
+            act_slot(t, h), act_slot(t, h), act_fwd.at[t, h, q], act_recv.at[t, h], (s, to)
+        ))
 
     def act_pass(run):
+        def others(body):
+            def step(i):
+                t = layer_of(i // inner) * inner + i % inner
+
+                @pl.when(t != s)
+                def _():
+                    body(t)
+            loop(0, n, step)
+
         for h, root in ((0, root_a), (1, root_b)):
             @pl.when(m == root)
             def _():
-                for k in range(1, n):
-                    t = (s + k) % n
+                def first(t):
                     if run:
                         act_wait(t, h)
-                    for q, peer in enumerate(mp_peers):
-                        go(run, remote(
-                            act_slot(t, h), act_slot(t, h), act_fwd.at[t, q], act_recv.at[t, h], peer,
-                        ))
+                    act_send_on(run, t, h, opposite, 0)
+                    act_send_on(run, t, h, sibling, 1)
+                others(first)
+
+                def second(t):
+                    if run:
+                        act_wait(t, 1 - h)
+                    act_send_on(run, t, 1 - h, sibling, 1)
+                others(second)
+
+        @pl.when(m == root_b)
+        def _():
+            for h in range(2):
+                if run:
+                    act_wait(s, h)
+                act_send_on(run, s, h, sibling, 1)
 
     def act_rest():
-        for h, root in ((0, root_a), (1, root_b)):
-            @pl.when(m != root)
-            def _():
-                for k in range(1, n):
-                    act_wait((s + k) % n, h)
-
-            @pl.when(m != root_a)
-            def _():
-                act_wait(s, h)
+        @pl.when((m != root_a) & (m != root_b))
+        def _():
+            def step(t):
+                for h in range(2):
+                    act_wait(t, h)
+            loop(0, n, step)
 
         @pl.when(m == root_a)
         def _():
-            act_mine(s % per).wait()
-
-    def layer_of(k):
-        if k == 0:
-            return z
-        low = outer // 2
-        if k == 1:
-            return jnp.where(z < low, low - 1 - z, 3 * low - 1 - z)
-        return jnp.where(z < low, k, outer - 1 - k)
-
-    def sums(run, g):
-        for q, peer in enumerate(mp_peers):
-            part_copy(run, g, q, peer)
-
-    def part_copy(run, g, q, peer):
+            act_mine().wait()
+
+    def part_copy(run, i, q):
         go(run, remote(
-            terms.at[peer[1]], parts.at[g, m], rs_send.at[g, q], rs_recv.at[g, m], peer,
+            terms.at[i % 2, mp_peers[q][1]], parts.at[i * mp + m], rs_send.at[i, q], rs_recv.at[i, m], mp_peers[q],
         ))
 
-    def select(layer):
-        tile = 512 if quarter % 512 == 0 else quarter
-        for j in range(inner):
-            t = layer * inner + j
-
-            def step(c):
-                at = pl.ds(pl.multiple_of(c * tile, tile), tile)
-                picked[pl.ds(j * FRAME, FRAME), at] = jnp.dot(
-                    place_ref[pl.ds(pl.multiple_of(t * FRAME, FRAME), FRAME), :],
-                    rows_all[t, :, at], preferred_element_type=jnp.float32,
-                ).astype(jnp.bfloat16)
-            loop(0, quarter // tile, step)
-
-    def hidden(g, layer):
-        select(layer)
-        if g > 0:
-            sums(False, g - 1)
-        tile = 256 if width % 256 == 0 else width
+    def source(i, j):
+        return jnp.where(
+            edge,
+            jnp.where(i == 0, s, layer_of(jnp.maximum(i - 1, 0)) * inner + j),
+            layer_of(i) * inner + j,
+        )
+
+    def hidden(i):
+        @pl.when(i >= 2)
+        def _():
+            for q in range(mp - 1):
+                part_copy(False, i - 2, q)
+        tile = 256 if quarter % 256 == 0 else quarter
+
+        def choose(c):
+            at = pl.ds(pl.multiple_of(c * tile, tile), tile)
+            found = []
+            for j in range(inner):
+                t = source(i, j)
+                rows = rows_all[t // inner, pl.ds(pl.multiple_of((t % inner) * size, 16), size), at]
+                found.append(jnp.dot(
+                    place_ref[pl.ds(pl.multiple_of((i * inner + j) * FRAME, FRAME), FRAME), :],
+                    rows, preferred_element_type=jnp.float32,
+                ))
+            picked[at, :] = jnp.concatenate(found, axis=0).T.astype(jnp.bfloat16)
+        loop(0, quarter // tile, choose)
+        block_rows = 256 if width % 256 == 0 else width
         for q in range(mp):
             to = (m + 1 + q) % mp
 
             def step(c):
-                col = pl.multiple_of(c * tile, tile)
-                value = lax.dot_general(
-                    picked[...], w_all[pl.ds(pl.multiple_of(to * width + c * tile, tile), tile), :],
-                    (((1,), (1,)), ((), ())), preferred_element_type=jnp.float32,
+                col = pl.multiple_of(c * block_rows, block_rows)
+                value = jnp.dot(
+                    w_all[pl.ds(pl.multiple_of(to * width + c * block_rows, block_rows), block_rows), :],
+                    picked[...], preferred_element_type=jnp.float32,
                 ).astype(jnp.bfloat16)
                 if q < mp - 1:
-                    terms[to, :, pl.ds(col, tile)] = value
+                    terms[i % 2, to, pl.ds(col, block_rows), :] = value
                 else:
-                    parts[g, m, :, pl.ds(col, tile)] = value
-            loop(0, width // tile, step)
+                    parts[i * mp + m, pl.ds(col, block_rows), :] = value
+            loop(0, width // block_rows, step)
             if q > 0:
-                part_copy(True, g, q - 1, mp_peers[q - 1])
-
-    def reduce(g, layer):
+                part_copy(True, i, q - 1)
+
+    def reduce(i):
         for q, peer in enumerate(mp_peers):
             remote(
-                terms.at[0], parts.at[g, peer[1]], rs_send.at[g, q], rs_recv.at[g, peer[1]], peer
+                terms.at[0, 0], parts.at[i * mp + peer[1]], rs_send.at[i, q], rs_recv.at[i, peer[1]], peer
             ).wait_recv()
         tile = 256 if width % 256 == 0 else width
+
+        def step(c):
+            at = pl.ds(pl.multiple_of(c * tile, tile), tile)
+            total = parts[i * mp, at, :].astype(jnp.float32)
+            for q in range(1, mp):
+                total = total + parts[i * mp + q, at, :].astype(jnp.float32)
+            total = total.T.astype(jnp.bfloat16)
+            for j in range(inner):
+                t = jnp.where(edge & (i == 0), n + j, source(i, j))
+                hid[t, :, at] = total[j * FRAME:(j + 1) * FRAME]
+        loop(0, width // tile, step)
+
+        @pl.when(edge & (i == 0))
+        def _():
+            far(True)
+
+    def far(run):
         for j in range(inner):
-            t = layer * inner + j
-
-            def step(c):
-                at = pl.ds(pl.multiple_of(c * tile, tile), tile)
-                rows = pl.ds(j * FRAME, FRAME)
-                total = parts[g, 0, rows, at].astype(jnp.float32)
-                for q in range(1, mp):
-                    total = total + parts[g, q, rows, at].astype(jnp.float32)
-                hid[t, :, at] = total.astype(jnp.bfloat16)
-            loop(0, width // tile, step)
-
-    def line_up(layer):
+            go(run, remote(
+                hid.at[n + j], hid.at[s], far_send.at[j], far_recv.at[xi],
+                ((outer - 1 - z) * inner + j, m),
+            ))
+
+    def far_wait():
+        for j in range(inner):
+            t = (outer - 1 - z) * inner + j
+            remote(hid.at[t], hid.at[t], far_send.at[j], far_recv.at[j], seq_peers[0]).wait_recv()
+
+    def line_up(k):
+        layer = layer_of(k)
         for j in range(inner):
             t = layer * inner + j
 
@@ -678,14 +747,14 @@
 
             def step(c):
                 at = pl.ds(pl.multiple_of(c * 128, 128), 128)
-                lined[j, at, :] = lax.dot_general(
+                lined[k % 2, at, pl.ds(j * size, size)] = lax.dot_general(
                     block[:, at], hot[...], (((0,), (0,)), ((), ())),
                     preferred_element_type=jnp.float32,
                 ).astype(jnp.bfloat16)
             loop(0, kept // 128, step)
 
-    def weights(g, layer, last):
-        line_up(layer)
+    def weights(k):
+        layer = layer_of(k)
         tile = 256 if quarter % 256 == 0 else quarter
         count = quarter // tile
 
@@ -695,111 +764,147 @@
 
         def step(c):
             at = pl.ds(pl.multiple_of(c * tile, tile), tile)
-            value = jnp.dot(lined[0], rows_all[layer * inner, :, at], preferred_element_type=jnp.float32)
-            for j in range(1, inner):
-                value = value + jnp.dot(
-                    lined[j], rows_all[layer * inner + j, :, at], preferred_element_type=jnp.float32
-                )
-            if g > 0:
-                value = value + acc[:, at]
-            if not last:
+            value = acc[:, at] + jnp.dot(
+                lined[k % 2], rows_all[layer, :, at], preferred_element_type=jnp.float32
+            )
+
+            @pl.when(k < outer - 1)
+            def _():
                 acc[:, at] = value
-                return
-            slot = c % 2
-
-            @pl.when(c > 1)
-            def _():
-                put(c - 2, slot).wait()
-            stage[slot] = (value * factor).astype(jnp.bfloat16)
-            put(c, slot).start()
+
+            @pl.when(k == outer - 1)
+            def _():
+                slot = c % 2
+
+                @pl.when(c > 1)
+                def _():
+                    put(c - 2, slot).wait()
+                stage[slot] = (value * factor).astype(jnp.bfloat16)
+                put(c, slot).start()
         loop(0, count, step)
-        if last:
+
+        @pl.when(k < outer - 1)
+        def _():
+            line_up(k + 1)
+
+        @pl.when(k == outer - 1)
+        def _():
             for c in range(max(0, count - 2), count):
                 put(c, c % 2).wait()
 
+    def clear(c):
+        at = pl.ds(pl.multiple_of(c * 128, 128), 128)
+        acc[at, :] = jnp.zeros((128, quarter), jnp.float32)
+
     fetch = pltpu.make_async_copy(w_ref, w_all, w_sem)
-    keep = pltpu.make_async_copy(rows_ref, rows_all.at[s], local_sem.at[0])
+    keep = pltpu.make_async_copy(
+        rows_ref, rows_all.at[z, pl.ds(xi * size, size)], local_sem.at[0]
+    )
+    lead = min(4, pieces)
     act_first(True)
-    own_rows(True)
+    own_rows(True, 0, lead)
     keep.start()
     fetch.start()
-    partner_rows(True)
+    act_relay(True)
+    own_rows(True, lead, pieces)
+    loop(0, kept // 128, clear)
+    loop(0, early, lambda p: partner_row(True, p))
     act_pass(True)
-    hop(True, 1, 0, pieces)
     keep.wait()
     fetch.wait()
-    rest(layer_of(0))
-    hidden(0, layer_of(0))
-    rest(layer_of(1))
-    act_rest()
-    weights(0, layer_of(0), False)
-    reduce(0, layer_of(0))
-    hidden(1, layer_of(1))
-    weights(1, layer_of(1), False)
-    hop(True, 2, 0, pieces)
-    rest(layer_of(2))
-    reduce(1, layer_of(1))
-    hidden(2, layer_of(2))
-    weights(2, layer_of(2), False)
-    hop(True, 3, 0, pieces)
-    rest(layer_of(3))
-    reduce(2, layer_of(2))
-    hidden(3, layer_of(3))
-    weights(3, layer_of(3), True)
-    reduce(3, layer_of(3))
+
+    def since(e, *steps):
+        total = 0
+        for at in steps:
+            total = total + jnp.where(e >= at, 1, 0)
+        return total
+
+    middle = pieces // 2
+
+    def stage_of(e):
+        late = e % 2
+        hop(True, 1 + e // 2, late * middle, jnp.where(late == 1, pieces, middle))
+        terms_from, terms_to = since(e, 1, 3, 4, 5), since(e, 0, 2, 3, 4)
+        grad_from, grad_to = since(e, 2, 4, 5, 6), since(e, 1, 3, 4, 5)
+        loop(jnp.where(edge, grad_from, terms_from), jnp.where(edge, grad_to, terms_to), rest)
+        loop(since(e, 3, 4, 6, 6), since(e, 2, 3, 5, 5), reduce)
+        loop(terms_from, terms_to, hidden)
+
+        @pl.when(e == 1)
+        def _():
+            act_rest()
+            line_up(0)
+        loop(grad_from, grad_to, weights)
+
+    loop(0, 2 * (outer - 1), stage_of)
+
+    @pl.when(edge)
+    def _():
+        far_wait()
     for f in range(frames):
         hid_out[pl.ds(f * FRAME, FRAME), :] = hid[order_ref[n * frames + f]]
 
     act_first(False)
-    own_rows(False)
-    sums(False, outer - 1)
-    partner_rows(False)
-    for d in range(1, outer):
-        hop(False, d, 0, pieces)
+    act_relay(False)
+    own_rows(False, 0, pieces)
+    for i in range(outer - 2, outer):
+        for q in range(mp - 1):
+            part_copy(False, i, q)
+    loop(0, early, lambda p: partner_row(False, p))
+    loop(1, outer, lambda d: hop(False, d, 0, pieces))
     act_pass(False)
 
-
-def fused(n, mp, tag, factor, order, rows, acts, place, taken, w_out):
+    @pl.when(edge)
+    def _():
+        far(False)
+
+
+def fused(n, mp, grain, early, tag, factor, order, rows, acts, place, taken, w_out):
     stripe, quarter = rows.shape
     per, frames, _, kept = acts.shape
     width = w_out.shape[0] // mp
     inner = n // 4
     outer = n // inner
-    pieces = stripe // 32
+    pieces = stripe // grain
     vm = pl.BlockSpec(memory_space=pltpu.VMEM)
     anywhere = pl.BlockSpec(memory_space=pl.ANY)
     dma = pltpu.SemaphoreType.DMA
     b16 = jnp.bfloat16
     return pl.pallas_call(
-        functools.partial(fused_kernel, n, mp, inner, pieces, 1, factor),
+        functools.partial(fused_kernel, n, mp, inner, pieces, early, factor),
         out_shape=(
             jax.ShapeDtypeStruct((frames * FRAME, width), b16),
             jax.ShapeDtypeStruct((kept, quarter), b16),
         ),
-        in_specs=[pl.BlockSpec(memory_space=pltpu.SMEM)] + [vm] * 4 + [anywhere],
+        in_specs=[pl.BlockSpec(memory_space=pltpu.SMEM), anywhere, anywhere, vm, vm, anywhere],
         out_specs=(vm, anywhere),
         scratch_shapes=[
-            pltpu.VMEM((n, stripe, quarter), b16),
+            pltpu.VMEM((outer, inner * stripe, quarter), b16),
             pltpu.VMEM((n * frames, FRAME, kept), b16),
+            pltpu.VMEM((per, frames // 2, FRAME, kept), b16),
             pltpu.VMEM(w_out.shape, b16),
             pltpu.VMEM((kept, quarter), jnp.float32),
             pltpu.VMEM((frames * FRAME, stripe), b16),
             pltpu.VMEM((frames * FRAME, kept), b16),
-            pltpu.VMEM((inner, kept, stripe), b16),
-            pltpu.VMEM((inner * FRAME, quarter), b16),
-            pltpu.VMEM((mp, inner * FRAME, width), b16),
-            pltpu.VMEM((outer, mp, inner * FRAME, width), b16),
-            pltpu.VMEM((n, FRAME, width), b16),
+            pltpu.VMEM((2, kept, inner * stripe), b16),
+            pltpu.VMEM((quarter, inner * FRAME), b16),
+            pltpu.VMEM((2, mp, width, inner * FRAME), b16),
+            pltpu.VMEM((outer * mp, width, inner * FRAME), b16),
+            pltpu.VMEM((n + inner, FRAME, width), b16),
             pltpu.VMEM((2, kept, 256 if quarter % 256 == 0 else quarter), b16),
             dma(()), dma((outer, mp)), dma((outer, mp)),
             dma((n, pieces)), dma((n, pieces, 3)),
-            dma((n, 2)), dma((per, 2)), dma((n, mp)), dma((2, mp)),
+            dma((n, 2)), dma((per,)), dma((n, 2, 2)), dma((2, 2)),
+            dma((per,)), dma((per,)), dma((per,)), dma((inner,)), dma((inner,)),
             dma((2,)), dma((2,)),
         ],
         compiler_params=pltpu.CompilerParams(
             collective_id=tag, has_side_effects=True, vmem_limit_bytes=67043328
         ),
     )(order, rows, acts, place, taken, w_out)
+
+
+GRAIN, EARLY = 32, 1
 
 
 def local_fused(n, mp, grad_rows, img_start, img_len, img_owner, pre_act, w_out):
@@ -824,9 +929,22 @@
     my_start = lax.dynamic_slice_in_dim(starts, here, 1)[0] - here * stripe
     my_length = lax.dynamic_slice_in_dim(lengths, here, 1)[0]
     my_before = lax.dynamic_slice_in_dim(before, here, 1)[0]
+    inner, outer = n // 4, 4
+    z = here // inner
+    edge = (z == 0) | (z == outer - 1)
+    step = jnp.arange(n, dtype=jnp.int32) // inner
+    side = jnp.arange(n, dtype=jnp.int32) % inner
+    k = jnp.where(edge, jnp.maximum(step - 1, 0), step)
+    mate = jnp.where(z < outer // 2, outer // 2 - 1 - z, 3 * outer // 2 - 1 - z)
+    layer = jnp.where(k == 0, z, jnp.where(k == 1, mate, jnp.where(z < outer // 2, k, outer - 1 - k)))
+    distant = edge & (step == 0)
+    from_stripe = jnp.where(distant, here, layer * inner + side)
+    to_owner = jnp.where(distant, (outer - 1 - z) * inner + side, here)
     mine = (owner == here).astype(jnp.int32)
-    first = jnp.sum(mine * before, axis=1)
-    count = jnp.sum(mine * lengths, axis=1)
+    match = (from_stripe[:, None, None] == jnp.arange(n, dtype=jnp.int32)[None, :, None])
+    match = (match & (owner[None] == to_owner[:, None, None])).astype(jnp.int32)
+    first = jnp.sum(match * before[None], axis=(1, 2))
+    count = jnp.sum(match * lengths[None], axis=(1, 2))
     at = jnp.where(row[None, :] < count[:, None], first[:, None] + row[None, :], -1).reshape(n * FRAME, 1)
     source_of = jnp.sum(mine * jnp.arange(n, dtype=jnp.int32)[:, None], axis=0)
     order = img_owner * frames + jnp.arange(n * frames, dtype=jnp.int32) % frames
@@ -840,7 +958,7 @@
         rows = jnp.dot(live, grad_rows, preferred_element_type=jnp.float32).astype(jnp.bfloat16)
         place = (at == jnp.arange(size, dtype=jnp.int32)[None, :]).astype(jnp.bfloat16)
         taken = spread(lengths, before, block, size).reshape(n, 1, size)
-        return fused(n, mp, tag, factor, order, rows, acts, place, taken, w_out)
+        return fused(n, mp, GRAIN, EARLY, tag, factor, order, rows, acts, place, taken, w_out)
 
     sizes = [stripe // 16 * k for k in (12, 13, 16)]
     most = jnp.max(jnp.sum(lengths, axis=1))
@@ -856,7 +974,7 @@
 
 def chosen(n, mp, grad_rows, *rest):
     whole = n * grad_rows.shape[0] * grad_rows.shape[1] + rest[-1].shape[0] * rest[-1].shape[1]
-    fits = n * FRAME == grad_rows.shape[0] and 2 * whole <= 40 * 1024 * 1024
+    fits = n * FRAME == grad_rows.shape[0] and n == 2 * mp and 2 * whole <= 40 * 1024 * 1024
     return (local_fused if fits else local)(n, mp, grad_rows, *rest)
 
 

time: 289 us -> 203 us (0.70); the launches traced: 286 us -> 203 us
  Pallas kernels: 257 us -> 183 us
  loops' own time: 9.81 us -> 0.32 us
    pallas_call x1, Pallas kernels: 257 us -> 183 us  [fused(): pl.pallas_call(functools.partial(fused_kernel, n, mp, inner, pieces, earl...]
    unnamed x1, loops' own time: 9.81 us -> 0.32 us
where the time goes in v1:
time: 203 us
  Pallas kernels  183 us (90%)
  other arithmetic  9.51 us (5%)
  local copies, waits for them, and re-layouts  5.31 us (3%)
  matrix products  2.17 us (1%)
  between operations  2.05 us (1%)
    pallas_call x1, Pallas kernels, fused(): pl.pallas_call(functools.partial(fused_kernel, n, mp, inner, pieces, earl...  183 us

profile of v1, /device:TPU:0, one launch (start us, length us, event | category | flops | bytes accessed | tf_op | source)
XLA Modules:
  0.0 202.6 jit_solution(14998710293486770016)
XLA Ops:
  0.7 0.7 fusion.27
  1.3 0.1 iota_compare_fusion.15
  1.4 0.7 reshape.239
  2.1 0.2 reduce_window_sum.11
  2.3 0.7 eq.186
  3.1 0.6 pad_add_fusion
  3.7 0.1 compare_and_fusion
  3.8 0.1 lt.161
  3.9 0.1 fusion.31
  4.0 0.6 reduce_max.9
  5.9 0.0 copy-start.1
  5.9 0.0 copy-start.2
  6.0 0.0 copy-start.3
  6.0 2.1 %fusion.21 = bf16[512,1280]{1,0:T(8,128)(2,1)S(1)} fusion(bf16[512,1280]{1,0:T(8,128)(2,1)} %param.13), kind=kLoop, calls=%fused_computation.77 | loop fusion | flops 3932160 | bytes 2621440 | tf_op jit(solution)/shard_map/convert_element_type | solution.py:926
  8.1 1.2 copy.12
  9.2 0.0 copy-done.1
  9.2 188.3 %conditional.2 = (bf16[640,2048]{1,0:T(8,128)(2,1)}, bf16[512,1280]{1,0:T(8,128)(2,1)}) conditional(s32[]{:T(128)} %clamp.3, (s32[1,8]{1,0:T(1,128)S(1)}, s32[8,8]{1,0:T(8,128)S(1)}, s32[]{:T(128)}, s32[64]{0:T(128)S(1)}, s32[]{:T(128)}, /*index=5*/s32[512]{0:T(512)S(1)}, bf16[512,2048]{1,0:T(8,128)(2,1)S(1)}, ...), branch_computations={%region_4.9_spmd, %region_9.14_spmd, %region_14.19_spmd} | conditional | flops 1075838592 | bytes 4842500
  9.3 0.1 reshape.228
  9.4 0.1 select_reduce_fusion.3
  9.5 0.1 reshape.230
  9.5 0.4 select_reduce_fusion.1
  9.9 0.1 add.244
  10.0 0.1 add.245
  10.1 0.1 select_reduce_fusion
  10.2 0.6 sub.107.taken_ref
  10.8 0.1 lt.121
  10.9 0.1 lt.122
  11.0 0.9 fusion.place_ref
  11.9 2.2 %convolution_convert_fusion.rows_ref = bf16[384,2048]{1,0:T(8,128)(2,1)} fusion(bf16[512,2048]{1,0:T(8,128)(2,1)S(1)} %get-tuple-element.413, s32[512]{0:T(512)S(1)} %get-tuple-element.412, s32[384]{0:T(512)S(1)} %broadcast_add_fusion.1), kind=kOutput, calls=%fused_computation | convolution fusion | flops 806289408 | bytes 3673600 | tf_op jit(solution)/shard_map/cond/branch_0_fun/dot_general | solution.py:958
  14.0 183.2 %branch_0_fun.2 = (bf16[512,1280]{1,0:T(8,128)(2,1)}, bf16[640,2048]{1,0:T(8,128)(2,1)}) custom-call(s32[72]{0:T(128)} %get-tuple-element.406.order_ref, bf16[384,2048]{1,0:T(8,128)(2,1)} %convolution_convert_fusion.rows_ref, bf16[2,8,64,640]{3,2,1,0:T(8,128)(2,1)} %bitcast.3.act_ref, bf16[512,384]{1,0:T(8,128)(2,1)} %fusion.place_ref, ...), custom_call_target="tpu_custom_call" | custom-call | tf_op jit(solution)/shard_map/cond/branch_0_fun/pallas_call | solution.py:873
  197.6 3.5 %fusion.26 = bf16[512,1280]{1,0:T(8,128)(2,1)} fusion(bf16[512,1280]{1,0:T(8,128)(2,1)} %param.13, bf16[512,1280]{1,0:T(8,128)(2,1)} %get-tuple-element.470), kind=kLoop, calls=%fused_computation.82 | loop fusion | flops 7864320 | bytes 3932160 | tf_op jit(solution)/shard_map/convert_element_type | solution.py:971
  201.1 1.5 copy.20
  (18 shorter events, 0.1 us)
Async XLA Ops:
  5.9 3.3 %copy-start.1 = (s32[64]{0:T(128)S(1)}, s32[64]{0:T(128)}, u32[]{:S(2)}) copy-start(s32[64]{0:T(128)} %param.11) | copy-start | bytes 772
  5.9 3.3 %copy-start.2 = (s32[64]{0:T(128)S(1)}, s32[64]{0:T(128)}, u32[]{:S(2)}) copy-start(s32[64]{0:T(128)} %param.10) | copy-start | bytes 772
  6.0 3.3 %copy-start.3 = (bf16[512,2048]{1,0:T(8,128)(2,1)S(1)}, bf16[512,2048]{1,0:T(8,128)(2,1)}, u32[]{:S(2)}) copy-start(bf16[512,2048]{1,0:T(8,128)(2,1)} %param.9) | copy-start | bytes 6291460
  197.6 3.5 %copy-start = (bf16[640,2048]{1,0:T(8,128)(2,1)S(1)}, bf16[640,2048]{1,0:T(8,128)(2,1)}, u32[]{:S(2)}) copy-start(bf16[640,2048]{1,0:T(8,128)(2,1)} %get-tuple-element.503) | copy-start | bytes 7864324
